TPU v7x, 128 devices: a whole 4x4x4 slice. The times are simulated.
128 devices in a mesh: gx: 4 (over x), gy: 4 (over y_lo, core), gz: 8 (over z, y_hi).
Axes of the slice: x: 4, y: 4 (y_hi: 2, y_lo: 2; y = y_hi * 2 + y_lo), z: 4, core: 2. Of those that a mesh axis runs over, the one named last changes fastest.
Arguments:
- grad_bucket: bfloat16 [128, 1, 3584, 1024], P(('gx', 'gy', 'gz')), may hold values from -72000 to 72000
- parameters: bfloat16 [1, 3584, 1024], P(None, ('gx', 'gy', 'gz')), may hold values from -4 to 4
- row_state: float32 [1, 3584], P(None, ('gx', 'gy', 'gz')), may hold values from 0.01 to 10
- column_state: float32 [1, 1024], replicated, may hold values from 0.01 to 10
Outputs:
- new_parameters: bfloat16 [1, 3584, 1024], P(None, ('gx', 'gy', 'gz'))
- row_next: float32 [1, 3584], P(None, ('gx', 'gy', 'gz'))
- column_next: float32 [1, 1024], replicated
- first_layer: bfloat16 [3584, 1024], replicated
All inputs are finite; a program needn't handle non-finite values.
Results may differ from a plain program's by a relative error of at most 0.011.
Values may be sent and summed in bfloat16 or wider, within the bound.
A program may use at most 128 MiB of HBM per device.

v0:
```python
import math

import jax.numpy as jnp
from jax import lax

D = 3584
LAYERS = 1
KW = 1024


beta_two = 0.8


step_size = 0.5


def reference(grad_bucket, parameters, row_state, column_state):

    def accumulate(running, device_grad):
        return (running + device_grad.astype(jnp.float32), None)

    summed, unused = lax.scan(accumulate, jnp.zeros((LAYERS, D, KW), jnp.float32), grad_bucket)
    norm_square = jnp.sum(summed * summed)
    clip_level = 0.5 * math.sqrt(LAYERS * D * KW)
    factor = jnp.minimum(jnp.float32(1.0), clip_level / jnp.sqrt(norm_square + 1e-06))
    clipped = factor * summed
    squares = clipped * clipped
    row_next = beta_two * row_state + (1.0 - beta_two) * jnp.mean(squares, axis=2)
    column_next = beta_two * column_state + (1.0 - beta_two) * jnp.mean(squares, axis=1)
    row_average = jnp.mean(row_next, axis=1)
    second = row_next[:, :, None] * column_next[:, None, :] / row_average[:, None, None]
    update = clipped / jnp.sqrt(second)
    new_parameters = (parameters.astype(jnp.float32) - step_size * update).astype(jnp.bfloat16)
    return (new_parameters, row_next, column_next, new_parameters[0])


def solution(mesh):
    return reference
```

profile of v0, /device:TPU:1, one launch (start us, length us, event | category | flops | bytes accessed | tf_op | source)
XLA Modules:
  0.0 716.8 jit_solution(11958846115376618924)
XLA Ops:
  7.2 10.9 %reshape.129 = bf16[1,1,128,28,1024]{4,3,2,1,0:T(8,128)(2,1)} reshape(bf16[1,1,3584,1024]{3,2,1,0:T(8,128)(2,1)} %param.3) | data formatting | bytes 14680064 | tf_op jit(solution)/call_exported
  18.1 11.9 %all-to-all-start = ((bf16[1,1,128,28,1024]{4,3,1,0,2:T(8,128)(2,1)}), bf16[1,1,128,28,1024]{4,3,1,0,2:T(8,128)(2,1)}, u32[]{:S(2)}, u32[]{:S(2)}) async-start(bf16[1,1,128,28,1024]{4,3,1,0,2:T(8,128)(2,1)} %bitcast.18), calls=%async_computation | async-start | bytes 16777216 | tf_op jit(solution)/call_exported
  30.1 104.1 %all-to-all-done = bf16[1,1,128,28,1024]{4,3,1,0,2:T(8,128)(2,1)} async-done(((bf16[1,1,128,28,1024]{4,3,1,0,2:T(8,128)(2,1)}), bf16[1,1,128,28,1024]{4,3,1,0,2:T(8,128)(2,1)}, u32[]{:S(2)}, u32[]{:S(2)}) %all-to-all-start) | async-done | bytes 7340064 | tf_op jit(solution)/call_exported
  134.2 114.8 %while.14 = (s32[]{:T(128)}, f32[1,28,1024]{2,1,0:T(8,128)S(1)}, bf16[1,1,3584,1024]{3,2,1,0:T(8,128)(2,1)}, bf16[1,1,128,28,1024]{4,3,2,1,0:T(8,128)(2,1)}, s32[]{:T(128)}, /*index=5*/s32[]{:T(128)}) while((s32[]{:T(128)}, f32[1,28,1024]{2,1,0:T(8,128)S(1)}, bf16[1,1,3584,1024]{3,2,1,0:T(8,128)(2,1)}, ...), condition=%wide.wide.region_1.2_spmd.clone, body=%wide.wide.region_0.1_spmd.clone.sunk | while | flops 86019 | bytes 286811 | solution.py:22
  135.1 0.9 convert_add_fusion.2
  136.0 0.9 convert_add_fusion.2
  142.3 0.9 convert_add_fusion.2
  143.1 0.9 convert_add_fusion.2
  144.0 0.9 convert_add_fusion.2
  144.9 0.9 convert_add_fusion.2
  150.3 0.9 convert_add_fusion.2
  151.2 0.9 convert_add_fusion.2
  152.1 0.9 convert_add_fusion.2
  153.0 0.9 convert_add_fusion.2
  159.3 0.9 convert_add_fusion.2
  160.2 0.9 convert_add_fusion.2
  161.1 0.9 convert_add_fusion.2
  162.0 0.9 convert_add_fusion.2
  249.6 64.7 %all-reduce = f32[]{:T(128)} all-reduce(f32[]{:T(128)} %multiply_reduce_fusion), channel_id=2, replica_groups=mesh['gx'=4,'gy'=4,'gz'=8] {'gx','gy','gz'}, use_global_device_ids=true, to_apply=%region_2.3.clone | all-reduce | flops 1 | bytes 8 | tf_op jit(solution)/reduce_sum | solution.py:23
  316.0 63.7 %all-reduce.3 = (f32[]{:T(128)}, f32[1024]{0:T(1024)S(1)}) all-reduce(f32[]{:T(128)} %get-tuple-element.71, f32[1024]{0:T(1024)S(1)} %get-tuple-element.59), channel_id=4, replica_groups=mesh['gx'=4,'gy'=4,'gz'=8] {'gx','gy','gz'}, use_global_device_ids=true, to_apply=%region_5.6.clone | all-reduce | flops 1025 | bytes 8200 | tf_op jit(solution)/reduce_sum | solution.py:30
  380.3 1.0 fusion.1
  381.3 1.6 copy.9
  382.9 315.8 %all-gather.4.cloned.1.call-done = bf16[1,3584,1024]{2,0,1:T(2,128)(2,1)} async-done(((bf16[1,28,1024]{2,0,1:T(2,128)(2,1)}), bf16[1,3584,1024]{2,0,1:T(2,128)(2,1)}) %all-gather.4.cloned.1.call-update) | async-done | bytes 7340048 | tf_op jit(solution)/squeeze | solution.py:34
  698.7 11.3 %copy.19 = bf16[1,3584,1024]{2,1,0:T(8,128)(2,1)} copy(bf16[1,3584,1024]{2,0,1:T(2,128)(2,1)} %all-gather.4.cloned.1.call-done) | data formatting | bytes 14680064
  (132 shorter events, 101.6 us)
Async XLA Ops:
  18.1 297.3 %copy-start.4 = (f32[1,28]{1,0:T(1,128)S(1)}, f32[1,28]{1,0:T(1,128)}, u32[]{:S(2)}) copy-start(f32[1,28]{1,0:T(1,128)} %param.4) | copy-start | bytes 340
  18.1 362.2 %copy-start.2 = (f32[1,1024]{1,0:T(1,128)S(1)}, f32[1,1024]{1,0:T(1,128)}, u32[]{:S(2)}) copy-start(f32[1,1024]{1,0:T(1,128)} %param.5) | copy-start | bytes 12292
  18.1 362.3 %copy-start = (bf16[1,28,1024]{2,1,0:T(8,128)(2,1)S(1)}, bf16[1,28,1024]{2,1,0:T(8,128)(2,1)}, u32[]{:S(2)}) copy-start(bf16[1,28,1024]{2,1,0:T(8,128)(2,1)} %param.2) | copy-start | bytes 172036
  18.1 116.1 %all-to-all-start = ((bf16[1,1,128,28,1024]{4,3,1,0,2:T(8,128)(2,1)}), bf16[1,1,128,28,1024]{4,3,1,0,2:T(8,128)(2,1)}, u32[]{:S(2)}, u32[]{:S(2)}) async-start(bf16[1,1,128,28,1024]{4,3,1,0,2:T(8,128)(2,1)} %bitcast.18), calls=%async_computation | async-start | bytes 16777216 | tf_op jit(solution)/call_exported
  30.0 668.7 %all-gather.4.cloned.1.call-start = ((), (), s32[]{:S(2)}) async-start(), calls=%async_computation.1 | async-start | bytes 14794752 | tf_op jit(solution)/squeeze | solution.py:34
  316.0 394.0 %copy-start.3 = (f32[1,28]{1,0:T(1,128)}, f32[1,28]{1,0:T(1,128)S(1)}, u32[]{:S(2)}) copy-start(f32[1,28]{1,0:T(1,128)S(1)} %get-tuple-element.72) | copy-start | bytes 340
  380.3 329.6 %copy-start.1 = (f32[1,1024]{1,0:T(1,128)}, f32[1,1024]{1,0:T(1,128)S(1)}, u32[]{:S(2)}) copy-start(f32[1,1024]{1,0:T(1,128)S(1)} %multiply_add_fusion) | copy-start | bytes 12292
Sparse Core Ops, SparseCore 0:
  381.5 317.1 all-gather.3
where the time goes:
time: 723 us; the launch traced here: 717 us
  waiting for transfers between devices  420 us (58%)
  blocking collectives  128 us (18%)
  other arithmetic  115 us (16%)
  local copies, waits for them, and re-layouts  23.8 us (3%)
  between operations  15.4 us (2%)
  starting transfers between devices  12 us (2%)
    squeeze x1, waiting for transfers between devices, reference(): return (new_parameters, row_next, column_next, new_parameters[0])  316 us
    add x128, other arithmetic, accumulate(): return (running + device_grad.astype(jnp.float32), None)  112 us
    another operation x1, waiting for transfers between devices  104 us
    reduce_sum x1, blocking collectives, reference(): norm_square = jnp.sum(summed * summed)  64.7 us
    reduce_sum x1, blocking collectives, reference(): row_average = jnp.mean(row_next, axis=1)  63.7 us
  transfers between devices with their start and end apart: 2, of which 2 were waited for; matrix products, arithmetic and copies ran while one was open for 0% of the time, Pallas kernels for 0%

commit v1 on v0

v1 whole, which is shorter than its diff:
```python
import math

import jax
import jax.numpy as jnp
from jax import lax
from jax.experimental import pallas as pl
from jax.experimental.pallas import tpu as pltpu
from jax.sharding import PartitionSpec as P

D = 3584
KW = 1024
CLIP = 0.5 * math.sqrt(D * KW)
BETA = 0.8
STEP = 0.5
MESH = pl.DeviceIdType.MESH
F32 = jnp.float32
BF16 = jnp.bfloat16

ORDER = ("xyz", "yzx", "zxy")
STRIP = ((0, 24), (24, 40), (40, 56))
ROWS = tuple(56 + b - a for a, b in STRIP)
LD, PR, RLP, RLM, FM, FP, SE, TH = 0, 4, 8, 12, 16, 20, 24, 27
GT, GS, GM, GP, GO, GC = 30, 33, 36, 40, 44, 48
NRECV = 49
NSEND = 8


def mod4(v):
    return lax.rem(v, 4)


def where_am_i():
    gx, gy, gz = lax.axis_index("gx"), lax.axis_index("gy"), lax.axis_index("gz")
    lo, core = lax.div(gy, 2), lax.rem(gy, 2)
    z, hi = lax.div(gz, 2), lax.rem(gz, 2)
    return {"x": gx, "y": 2 * hi + lo, "z": z}, lo, hi, core


def device(at, core):
    return (at["x"], lax.rem(at["y"], 2) * 2 + core, at["z"] * 2 + lax.div(at["y"], 2))


def pieces(t, a1):
    every = slice(None)
    if t == 0:
        return [((a1, every, None, every), h, (pl.ds(2 * h, 2), every)) for h in (0, 1)]
    if t == 1:
        hi, lo = lax.div(a1, 2), lax.rem(a1, 2)
        return [((every, lo, None, z), hi, (z, every)) for z in range(4)]
    return [((every, every, None, a1), h, (every, pl.ds(2 * h, 2))) for h in (0, 1)]


def rectangles(t):
    return [(t, 0, 56, 0), (3, STRIP[t][0], STRIP[t][1], 56)]


def copies(t, a1, core, whole, part):
    out = []
    for (x, lo, _, z), h, (i, j) in pieces(t, a1):
        for tile, r0, r1, d0 in rectangles(t):
            col = h * 512 + tile * 128
            if not isinstance(col, int):
                col = pl.multiple_of(col, 128)
            out.append((
                whole.at[x, lo, core, z, pl.ds(r0, r1 - r0), pl.ds(col, 128)],
                part.at[a1, i, j, pl.ds(d0, r1 - r0), :],
            ))
    return out


def step_kernel(*refs):
    (g, par_in, rs_in, cs_in), refs = refs[:4], refs[4:]
    outs, refs = refs[:9], refs[9:]
    own, other = outs[0:3], outs[3:6]
    newp, rown, coln = outs[6:9]
    it = iter(refs)
    take3 = lambda: [next(it) for _ in range(3)]
    w, pr, rlp, rlm, fm, fp, s1, r2, s2, r3, s3 = (take3() for _ in range(11))
    par, line, rs, cs, pf, px, pxr, rx, rxr, rq, rqr, st1, st2, st3 = (next(it) for _ in range(14))
    recv, send, xr, xs, t1r, t1s, t2r, t2s, near = (next(it) for _ in range(9))

    at, lo, hi, core = where_am_i()

    def moved(axis, k):
        to = dict(at)
        to[axis] = mod4(at[axis] + k)
        return to

    def push(src, dst, ssem, rsem, to, tc):
        pltpu.make_async_remote_copy(
            src_ref=src, dst_ref=dst, send_sem=ssem, recv_sem=rsem, device_id=device(to, tc), device_id_type=MESH
        ).start()

    def settle(ref, sem):
        pltpu.make_async_copy(ref, ref, sem).wait()

    axes = [tuple(ORDER[t]) for t in range(3)]
    pos = [tuple(at[a] for a in axes[t]) for t in range(3)]

    def rel(t, level, k):
        return mod4(pos[t][level] + k)

    small = ((par_in, par), (rs_in, line), (cs_in, cs))
    for i, (src, dst) in enumerate(small):
        pltpu.make_async_copy(src, dst, near.at[i]).start()
    for k in (2, 1, 3, 0):
        for t in range(3):
            for src, dst in copies(t, rel(t, 0, k), core, g, w[t]):
                pltpu.make_async_copy(src, dst, recv.at[t, LD + k]).start()

    barrier = pltpu.get_barrier_semaphore()
    for axis in "xyz":
        for k in (1, 2, 3):
            pl.semaphore_signal(barrier, inc=1, device_id=device(moved(axis, k), core), device_id_type=MESH)
    for k in range(4):
        pl.semaphore_signal(barrier, inc=1, device_id=device(moved("x", k), 1 - core), device_id_type=MESH)
    pl.semaphore_wait(barrier, 13)

    for k in (2, 1, 3, 0):
        for t in range(3):
            for src, (_, dst) in zip(
                [s for s, _ in copies(t, rel(t, 0, k), 1 - core, g, pr[t])], copies(t, rel(t, 0, k), core, g, pr[t])
            ):
                push(src, dst, send.at[t, 0], recv.at[t, PR + k], at, 1 - core)

    pf[...] = jnp.zeros_like(pf)
    for i, (src, dst) in enumerate(small):
        pltpu.make_async_copy(src, dst, near.at[i]).wait()
    wide = par[...].astype(F32)

    @pl.when(hi == 0)
    def _():
        pf[0:28, :] = wide

    @pl.when(hi == 1)
    def _():
        pf[28:56, :] = wide

    row_of = lax.broadcasted_iota(jnp.int32, (56, 128), 0)
    lane_of = lax.broadcasted_iota(jnp.int32, (56, 128), 1)
    on_diag = row_of == lane_of + 28 * hi
    rs[...] = jnp.zeros_like(rs)
    rs[0:1, 0:28] = line[...]
    rs_row = rs[0:1, :]
    rx[...] = jnp.where(on_diag & (lane_of < 28), jnp.broadcast_to(rs_row, (56, 128)), 0.0)
    px[...] = jnp.where(hi == 0, pf[:, 512:1024], pf[:, 0:512]).astype(BF16)
    mate = moved("y", 2)
    push(px, pxr, xs.at[0], xr.at[0], mate, core)
    push(rx, rxr, xs.at[1], xr.at[1], mate, core)

    def add_chunk(t, a1):
        settle(w[t].at[a1], recv_k[0])
        settle(pr[t].at[a1], recv_k[1])

        def body(i, carry):
            w[t][a1, i] = w[t][a1, i] + pr[t][a1, i]
            return carry

        lax.fori_loop(0, 4, body, 0)

    for k in (2, 1, 3, 0):
        for t in range(3):
            a1 = rel(t, 0, k)
            recv_k = (recv.at[t, LD + k], recv.at[t, PR + k])
            add_chunk(t, a1)
            up, down = moved(axes[t][0], 1), moved(axes[t][0], 3)
            if k == 2:
                for n, j in enumerate((2, 1)):
                    push(w[t].at[a1, rel(t, 1, j)], rlp[t].at[n], send.at[t, 1], recv.at[t, RLP + n], up, core)
                for n, j in enumerate((3, 0)):
                    push(w[t].at[a1, rel(t, 1, j)], rlm[t].at[n], send.at[t, 1], recv.at[t, RLM + n], down, core)
            if k == 1:
                for j in (3, 0):
                    push(w[t].at[a1, rel(t, 1, j)], fm[t].at[j], send.at[t, 1], recv.at[t, FM + j], up, core)
            if k == 3:
                for j in (2, 1):
                    push(w[t].at[a1, rel(t, 1, j)], fp[t].at[j], send.at[t, 1], recv.at[t, FP + j], down, core)

    for n in range(2):
        for t in range(3):
            up, down = moved(axes[t][0], 1), moved(axes[t][0], 3)
            for k, j, buf, base, dst, dbase, to in (
                (1, (2, 1)[n], rlp[t], RLP, fm[t], FM, up),
                (3, (3, 0)[n], rlm[t], RLM, fp[t], FP, down),
            ):
                settle(buf.at[n], recv.at[t, base + n])
                a1, a2 = rel(t, 0, k), rel(t, 1, j)
                w[t][a1, a2] = w[t][a1, a2] + buf[n]
                push(w[t].at[a1, a2], dst.at[j], send.at[t, 1], recv.at[t, dbase + j], to, core)

    for j in (2, 3, 1, 0):
        for t in range(3):
            settle(fm[t].at[j], recv.at[t, FM + j])
            settle(fp[t].at[j], recv.at[t, FP + j])
            a1, a2 = rel(t, 0, 0), rel(t, 1, j)

            def body(i, carry):
                s1[t][j, i] = (w[t][a1, a2, i].astype(F32) + fm[t][j, i].astype(F32) + fp[t][j, i].astype(F32)).astype(BF16)
                return carry

            lax.fori_loop(0, 4, body, 0)
            if j:
                push(s1[t].at[j], r2[t].at[j - 1], send.at[t, 2], recv.at[t, SE + j - 1], moved(axes[t][1], j), core)

    for t in range(3):
        for j in range(3):
            settle(r2[t].at[j], recv.at[t, SE + j])
        for m in (2, 1, 3, 0):
            a3 = rel(t, 2, m)
            total = s1[t][0, a3].astype(F32)
            for j in range(3):
                total = total + r2[t][j, a3].astype(F32)
            if m:
                s2[t][m - 1] = total.astype(BF16)
                push(s2[t].at[m - 1], r3[t].at[m - 1], send.at[t, 3], recv.at[t, TH + m - 1], moved(axes[t][2], m), core)
            else:
                s3[t][...] = total
    for t in range(3):
        total = s3[t][...]
        for m in range(3):
            settle(r3[t].at[m], recv.at[t, TH + m])
            total = total + r3[t][m].astype(F32)
        s3[t][...] = total

    tiles = [s3[t][0:56, :] for t in range(3)] + [jnp.concatenate([s3[t][56 : ROWS[t], :] for t in range(3)], axis=0)]
    squares = [v * v for v in tiles]
    rq[...] = squares[0] + squares[1] + squares[2] + squares[3]
    push(rq, rqr, xs.at[2], xr.at[2], mate, core)
    sums = [jnp.sum(v, axis=0, keepdims=True) for v in squares]
    eight = jnp.concatenate(sums + sums, axis=0)
    row8 = lax.broadcasted_iota(jnp.int32, (8, 128), 0)
    eight = jnp.where((row8 >= 4 * hi) & (row8 < 4 * hi + 4), eight, 0.0)
    mine = at["x"] * 2 + core
    st1[mine, 0:8, :] = eight
    st1[mine, 8:16, :] = rs[...]
    n = 0
    for k in range(4):
        for flip in (0, 1):
            if k or flip:
                tc = core if not flip else 1 - core
                push(st1.at[mine], st1.at[mine], t1s.at[0], t1r.at[n], moved("x", k), tc)
                n += 1
    n = 0
    for k in range(4):
        for flip in (0, 1):
            if k or flip:
                settle(st1.at[0], t1r.at[n])
                n += 1
    total = st1[0]
    for i in range(1, 8):
        total = total + st1[i]
    for level, (axis, buf) in enumerate((("y", st2), ("z", st3))):
        buf[at[axis]] = total
        for k in (2, 1, 3):
            push(buf.at[at[axis]], buf.at[at[axis]], t2s.at[level], t2r.at[level, k - 1], moved(axis, k), core)
        for k in (1, 3, 2):
            settle(buf.at[0], t2r.at[level, k - 1])
        total = buf[0] + buf[1] + buf[2] + buf[3]

    column_sums = total[0:8, :]
    norm_square = jnp.sum(jnp.sum(column_sums, axis=0, keepdims=True), axis=1, keepdims=True)
    rs_total = jnp.sum(total[8:9, :], axis=1, keepdims=True)
    factor = jnp.minimum(1.0, CLIP / jnp.sqrt(norm_square + 1e-06))
    square_factor = factor * factor
    column_next = BETA * cs[...] + (1.0 - BETA) * (square_factor * column_sums * (1.0 / D))
    coln[...] = column_next
    row_average = (BETA / D) * rs_total + (1.0 - BETA) * (square_factor * norm_square * (1.0 / (D * KW)))

    for i in range(3):
        settle((pxr, rxr, rqr)[i], xr.at[i])
    row_state = jnp.sum(rx[...] + rxr[...], axis=1, keepdims=True)
    row_square = jnp.sum(rq[...] + rqr[...], axis=1, keepdims=True)
    row_next = BETA * row_state + (1.0 - BETA) * (square_factor * row_square * (1.0 / KW))
    rown_line = jnp.sum(jnp.where(on_diag, jnp.broadcast_to(row_next, (56, 128)), 0.0), axis=0, keepdims=True)
    rown[...] = rown_line[:, 0:28]

    mine_half = jnp.where(hi == 0, column_next[0:4, :], column_next[4:8, :])
    fresh = []
    for tile in range(4):
        old = jnp.where(hi == 0, pf[:, tile * 128 : tile * 128 + 128], pf[:, 512 + tile * 128 : 640 + tile * 128])
        old = old + pxr[:, tile * 128 : tile * 128 + 128].astype(F32)
        second = row_next * mine_half[tile : tile + 1, :] / row_average
        update = factor * tiles[tile] / jnp.sqrt(second)
        fresh.append((old - STEP * update).astype(BF16))
    for t in range(3):
        a1, a2, a3 = pos[t]
        own[t][a1, a2, a3, 0:56, :] = fresh[t]
        own[t][a1, a2, a3, 56 : ROWS[t], :] = fresh[3][STRIP[t][0] : STRIP[t][1], :]

    for t in range(3):
        block = own[t].at[pos[t]]
        for k in (2, 1, 3):
            push(block, block, send.at[t, 4], recv.at[t, GT + k - 1], moved(axes[t][2], k), core)

    def arrived(t, j):
        sub = own[t].at[pos[t][0], rel(t, 1, j)]
        push(sub, sub, send.at[t, 6], recv.at[t, GM + j], moved(axes[t][0], 1), core)
        push(sub, sub, send.at[t, 6], recv.at[t, GP + j], moved(axes[t][0], 3), core)
        push(sub, other[t].at[pos[t][0], rel(t, 1, j)], send.at[t, 7], recv.at[t, GC], at, 1 - core)

    for t in range(3):
        for k in (1, 3, 2):
            settle(own[t].at[0, 0, 0], recv.at[t, GT + k - 1])
        sub = own[t].at[pos[t][0], pos[t][1]]
        for k in (2, 1, 3):
            push(sub, sub, send.at[t, 5], recv.at[t, GS + k - 1], moved(axes[t][1], k), core)
        arrived(t, 0)
    for j in (1, 3, 2):
        for t in range(3):
            settle(own[t].at[0, 0], recv.at[t, GS + (4 - j) - 1])
            arrived(t, j)

    for j in (0, 1, 3, 2):
        for t in range(3):
            for base, k, onward in ((GM, 3, 1), (GP, 1, 3)):
                sub = own[t].at[rel(t, 0, k), rel(t, 1, j)]
                settle(sub, recv.at[t, base + j])
                if (j in (0, 3)) == (onward == 1):
                    push(sub, sub, send.at[t, 6], recv.at[t, GO + j], moved(axes[t][0], onward), core)
                push(sub, other[t].at[rel(t, 0, k), rel(t, 1, j)], send.at[t, 7], recv.at[t, GC], at, 1 - core)
    for j in (0, 1, 3, 2):
        for t in range(3):
            sub = own[t].at[rel(t, 0, 2), rel(t, 1, j)]
            settle(sub, recv.at[t, GO + j])
            push(sub, other[t].at[rel(t, 0, 2), rel(t, 1, j)], send.at[t, 7], recv.at[t, GC], at, 1 - core)

    for h in (0, 1):
        here = dict(at, y=2 * h + lo)
        blocks = [own[t].at[tuple(here[a] for a in axes[t])] for t in range(3)]
        for t in range(3):
            pf[:, 512 * h + 128 * t : 512 * h + 128 * t + 128] = blocks[t][0:56, :].astype(F32)
            pf[STRIP[t][0] : STRIP[t][1], 512 * h + 384 : 512 * h + 512] = blocks[t][56 : ROWS[t], :].astype(F32)
    newp[...] = jnp.where(hi == 0, pf[0:28, :], pf[28:56, :]).astype(BF16)

    for t in range(3):
        settle(w[t], send.at[t, 0])
        settle(w[t].at[0:3], send.at[t, 1])
        settle(w[t].at[0, 0:3], send.at[t, 2])
        settle(w[t].at[0, 0, 0:3], send.at[t, 3])
        settle(w[t].at[0, 0, 0:3], send.at[t, 4])
        settle(w[t].at[0, 0:3], send.at[t, 5])
        settle(w[t].at[0:3], send.at[t, 6])
        settle(w[t], send.at[t, 7])
        settle(other[t], recv.at[t, GC])
    for i in range(3):
        settle((px, rx, rq)[i], xs.at[i])
    settle(st1.at[0:7], t1s.at[0])
    for level, buf in enumerate((st2, st3)):
        settle(buf.at[0:3], t2s.at[level])


def layout_kernel(*refs):
    own, other = refs[0:3], refs[3:6]
    newp, rown, coln = refs[6:9]
    whole, newp_out, rown_out, coln_out, sems = refs[9:]
    _, _, _, core = where_am_i()
    for src, dst in ((newp, newp_out), (rown, rown_out), (coln, coln_out)):
        pltpu.make_async_copy(src, dst, sems.at[3]).start()
    for held, c in ((own, core), (other, 1 - core)):
        for t in range(3):
            for a1 in range(4):
                for dst, src in copies(t, a1, c, whole, held[t]):
                    pltpu.make_async_copy(src, dst, sems.at[t]).start()
    for t in range(3):
        for held in (own, other):
            pltpu.make_async_copy(held[t], held[t], sems.at[t]).wait()
    for src, dst in ((newp, newp_out), (rown, rown_out), (coln, coln_out)):
        pltpu.make_async_copy(src, dst, sems.at[3]).wait()


def solution(mesh):
    block = [(r, 128) for r in ROWS]
    part = [jax.ShapeDtypeStruct((4, 4, 4) + b, BF16) for b in block]
    vmem = pl.BlockSpec(memory_space=pltpu.VMEM)
    anywhere = pl.BlockSpec(memory_space=pl.ANY)

    def local(grad_bucket, parameters, row_state, column_state):
        def three(*lead, dtype=BF16):
            return [pltpu.VMEM(lead + b, dtype) for b in block]

        scratch = (
            three(4, 4, 4) + three(4, 4, 4) + three(2, 4) + three(2, 4) + three(4, 4) + three(4, 4) + three(4, 4)
            + three(3, 4) + three(3) + three(3) + three(dtype=F32)
            + [
                pltpu.VMEM((28, KW), BF16), pltpu.VMEM((1, 28), F32), pltpu.VMEM((8, 128), F32), pltpu.VMEM((8, 128), F32),
                pltpu.VMEM((56, 1024), F32),
                pltpu.VMEM((56, 512), BF16), pltpu.VMEM((56, 512), BF16),
                pltpu.VMEM((56, 128), F32), pltpu.VMEM((56, 128), F32),
                pltpu.VMEM((56, 128), F32), pltpu.VMEM((56, 128), F32),
                pltpu.VMEM((8, 16, 128), F32), pltpu.VMEM((4, 16, 128), F32), pltpu.VMEM((4, 16, 128), F32),
                pltpu.SemaphoreType.DMA((3, NRECV)), pltpu.SemaphoreType.DMA((3, NSEND)),
                pltpu.SemaphoreType.DMA((3,)), pltpu.SemaphoreType.DMA((3,)),
                pltpu.SemaphoreType.DMA((7,)), pltpu.SemaphoreType.DMA((1,)),
                pltpu.SemaphoreType.DMA((2, 3)), pltpu.SemaphoreType.DMA((2,)),
                pltpu.SemaphoreType.DMA((3,)),
            ]
        )
        small = [
            jax.ShapeDtypeStruct((28, KW), BF16),
            jax.ShapeDtypeStruct((1, 28), F32),
            jax.ShapeDtypeStruct((8, 128), F32),
        ]
        held = pl.pallas_call(
            step_kernel,
            out_shape=part + part + small,
            in_specs=[pl.BlockSpec(memory_space=pltpu.HBM)] * 4,
            out_specs=[vmem] * 9,
            scratch_shapes=scratch,
            compiler_params=pltpu.CompilerParams(
                collective_id=0, has_side_effects=True, vmem_limit_bytes=40 * 1024 * 1024
            ),
            name="adafactor_step",
        )(
            grad_bucket.reshape(4, 2, 2, 4, 56, KW),
            parameters.reshape(28, KW),
            row_state,
            column_state.reshape(8, 128),
        )
        whole, newp, rown, coln = pl.pallas_call(
            layout_kernel,
            out_shape=[jax.ShapeDtypeStruct((4, 2, 2, 4, 56, KW), BF16)] + small,
            in_specs=[vmem] * 9,
            out_specs=[anywhere] * 4,
            scratch_shapes=[pltpu.SemaphoreType.DMA((4,))],
            compiler_params=pltpu.CompilerParams(vmem_limit_bytes=20 * 1024 * 1024),
            name="lay_out",
        )(*held)
        return newp.reshape(1, 28, KW), rown, coln.reshape(1, KW), whole.reshape(D, KW)

    every = ("gx", "gy", "gz")
    return jax.shard_map(
        local,
        mesh=mesh,
        in_specs=(P(every, None, None, None), P(None, every, None), P(None, every), P(None, None)),
        out_specs=(P(None, every, None), P(None, every), P(None, None), P(None, None)),
        check_vma=False,
    )
```

time: 723 us -> 70.5 us (0.10)
  waiting for transfers between devices: 420 us -> 0 us
  blocking collectives: 128 us -> 0 us
  other arithmetic: 115 us -> 0 us
  Pallas kernels: 0 us -> 67.4 us
  local copies, waits for them, and re-layouts: 23.8 us -> 2.17 us
  between operations: 15.4 us -> 0.65 us
  starting transfers between devices: 12 us -> 0 us
    squeeze x1 -> x0, waiting for transfers between devices: 316 us -> none  [reference(): return (new_parameters, row_next, column_next, new_parameters[0])]
    reduce_sum x2 -> x0, blocking collectives: 128 us -> none  [the longest x1 64.7 us: reference(): norm_square = jnp.sum(summed * summed)]
    add x129 -> x0, other arithmetic: 112 us -> none  [the longest x128 112 us: accumulate(): return (running + device_grad.astype(jnp.float32), None)]
    another operation x1 -> x0, waiting for transfers between devices: 104 us -> none
    pallas_call x0 -> x2, Pallas kernels: none -> 67.4 us  [the longest x1 64.5 us: local(): pl.pallas_call(step_kernel, out_shape=part + part + small, in_specs=[pl.B...]
    another operation x1 -> x0, starting transfers between devices: 11.9 us -> none
    another operation x1 -> x0, local copies, waits for them, and re-layouts: 10.9 us -> none
    unnamed x12 -> x6, local copies, waits for them, and re-layouts: 12.9 us -> 2.17 us
  transfers between devices with their start and end apart: 2 -> 0, of which waited for: 2 -> 0; matrix products, arithmetic and copies ran while one was open for 0% -> 0% of each run, Pallas kernels for 0% -> 0%
where the time goes in v1:
time: 70.5 us; the launch traced here: 70.3 us
  Pallas kernels  67.4 us (96%)
  local copies, waits for them, and re-layouts  2.17 us (3%)
    pallas_call x1, Pallas kernels, local(): pl.pallas_call(step_kernel, out_shape=part + part + small, in_specs=[pl.B...  64.5 us
    pallas_call x1, Pallas kernels, local(): pl.pallas_call(layout_kernel, out_shape=[jax.ShapeDtypeStruct((4, 2, 2, 4...  2.96 us
    unnamed x6, local copies, waits for them, and re-layouts  2.17 us

profile of v1, /device:TPU:1, one launch (start us, length us, event | category | flops | bytes accessed | tf_op | source)
XLA Modules:
  0.0 70.3 jit_solution(10078753407320224474)
XLA Ops:
  0.6 0.0 copy-start
  0.6 0.8 %copy-done = bf16[1,28,1024]{2,1,0:T(8,128)(2,1)S(1)} copy-done((bf16[1,28,1024]{2,1,0:T(8,128)(2,1)S(1)}, bf16[1,28,1024]{2,1,0:T(8,128)(2,1)}, u32[]{:S(2)}) %copy-start) | copy-done | bytes 57368
  1.5 0.0 copy-start.1
  1.5 0.7 copy-done.1
  2.2 0.0 copy-start.2
  2.2 0.7 copy-done.2
  2.8 64.5 %adafactor_step.1 = (bf16[4,4,4,80,128]{4,3,2,1,0:T(8,128)(2,1)S(1)}, bf16[4,4,4,72,128]{4,3,2,1,0:T(8,128)(2,1)S(1)}, bf16[4,4,4,72,128]{4,3,2,1,0:T(8,128)(2,1...) custom-call(bf16[4,2,2,4,56,1024]{5,4,3,2,1,0:T(8,128)(2,1)} %bitcas, ...), custom_call_target="tpu_custom_call" | custom-call | tf_op jit(solution)/shard_map/adafactor_step/pallas_call | solution.py:403
  67.3 3.0 %lay_out.1 = (bf16[4,2,2,4,56,1024]{5,4,3,2,1,0:T(8,128)(2,1)}, bf16[28,1024]{1,0:T(8,128)(2,1)}, f32[1,28]{1,0:T(1,128)}, f32[8,128]{1,0:T(8,128)}) custom-call(bf16[4,4,4,80,128]{4,3,2,1,0:T(8,128)(2,1)S(1)} %get-tuple-element.17.refs_0_, bf16[4,4,4,72,128]{4,3,2,1,0:T(8,128)(2,1)S(1)} %get-tuple-element.18.refs_1_, ...), custom_call_target="tpu_custom_call" | custom-call | tf_op jit(solution)/shard_map/lay_out/pallas_call | solution.py:419
Async XLA Ops:
  0.6 0.8 %copy-start = (bf16[1,28,1024]{2,1,0:T(8,128)(2,1)S(1)}, bf16[1,28,1024]{2,1,0:T(8,128)(2,1)}, u32[]{:S(2)}) copy-start(bf16[1,28,1024]{2,1,0:T(8,128)(2,1)} %param.5) | copy-start | bytes 172036
  1.5 0.7 copy-start.1
  2.2 0.7 copy-start.2

commit v2 on v1

--- a/solution.py
+++ b/solution.py
@@ -19,9 +19,9 @@
 ORDER = ("xyz", "yzx", "zxy")
 STRIP = ((0, 24), (24, 40), (40, 56))
 ROWS = tuple(56 + b - a for a, b in STRIP)
-LD, PR, RLP, RLM, FM, FP, SE, TH = 0, 4, 8, 12, 16, 20, 24, 27
-GT, GS, GM, GP, GO, GC = 30, 33, 36, 40, 44, 48
-NRECV = 49
+LD, PR, RLP, RLM, FM, FP, SE, TH = 0, 4, 8, 12, 16, 20, 24, 36
+GT, GS, GM, GP, GO, GC = 39, 42, 45, 49, 53, 57
+NRECV = 58
 NSEND = 8
 
 
@@ -76,7 +76,7 @@
     it = iter(refs)
     take3 = lambda: [next(it) for _ in range(3)]
     w, pr, rlp, rlm, fm, fp, s1, r2, s2, r3, s3 = (take3() for _ in range(11))
-    par, line, rs, cs, pf, px, pxr, rx, rxr, rq, rqr, st1, st2, st3 = (next(it) for _ in range(14))
+    par, line, rs, cs, pf, px, pxr, rx, rxr, rq, rqr, st1, st2 = (next(it) for _ in range(13))
     recv, send, xr, xs, t1r, t1s, t2r, t2s, near = (next(it) for _ in range(9))
 
     at, lo, hi, core = where_am_i()
@@ -110,11 +110,10 @@
 
     barrier = pltpu.get_barrier_semaphore()
     for axis in "xyz":
-        for k in (1, 2, 3):
+        for k in (1, 3):
             pl.semaphore_signal(barrier, inc=1, device_id=device(moved(axis, k), core), device_id_type=MESH)
-    for k in range(4):
-        pl.semaphore_signal(barrier, inc=1, device_id=device(moved("x", k), 1 - core), device_id_type=MESH)
-    pl.semaphore_wait(barrier, 13)
+    pl.semaphore_signal(barrier, inc=1, device_id=device(at, 1 - core), device_id_type=MESH)
+    pl.semaphore_wait(barrier, 7)
 
     for k in (2, 1, 3, 0):
         for t in range(3):
@@ -145,8 +144,6 @@
     rx[...] = jnp.where(on_diag & (lane_of < 28), jnp.broadcast_to(rs_row, (56, 128)), 0.0)
     px[...] = jnp.where(hi == 0, pf[:, 512:1024], pf[:, 0:512]).astype(BF16)
     mate = moved("y", 2)
-    push(px, pxr, xs.at[0], xr.at[0], mate, core)
-    push(rx, rxr, xs.at[1], xr.at[1], mate, core)
 
     def add_chunk(t, a1):
         settle(w[t].at[a1], recv_k[0])
@@ -165,50 +162,58 @@
             add_chunk(t, a1)
             up, down = moved(axes[t][0], 1), moved(axes[t][0], 3)
             if k == 2:
-                for n, j in enumerate((2, 1)):
-                    push(w[t].at[a1, rel(t, 1, j)], rlp[t].at[n], send.at[t, 1], recv.at[t, RLP + n], up, core)
-                for n, j in enumerate((3, 0)):
-                    push(w[t].at[a1, rel(t, 1, j)], rlm[t].at[n], send.at[t, 1], recv.at[t, RLM + n], down, core)
+                for j in (2, 3, 1, 0):
+                    sub = w[t].at[a1, rel(t, 1, j)]
+                    push(sub.at[0:2], rlp[t].at[j], send.at[t, 1], recv.at[t, RLP + j], up, core)
+                    push(sub.at[2:4], rlm[t].at[j], send.at[t, 1], recv.at[t, RLM + j], down, core)
             if k == 1:
-                for j in (3, 0):
-                    push(w[t].at[a1, rel(t, 1, j)], fm[t].at[j], send.at[t, 1], recv.at[t, FM + j], up, core)
+                for j in (2, 3, 1, 0):
+                    sub = w[t].at[a1, rel(t, 1, j)]
+                    push(sub.at[2:4], fm[t].at[j, 2:4], send.at[t, 1], recv.at[t, FM + j], up, core)
             if k == 3:
-                for j in (2, 1):
-                    push(w[t].at[a1, rel(t, 1, j)], fp[t].at[j], send.at[t, 1], recv.at[t, FP + j], down, core)
-
-    for n in range(2):
+                for j in (2, 3, 1, 0):
+                    sub = w[t].at[a1, rel(t, 1, j)]
+                    push(sub.at[0:2], fp[t].at[j, 0:2], send.at[t, 1], recv.at[t, FP + j], down, core)
+
+    for j in (2, 3, 1, 0):
         for t in range(3):
             up, down = moved(axes[t][0], 1), moved(axes[t][0], 3)
-            for k, j, buf, base, dst, dbase, to in (
-                (1, (2, 1)[n], rlp[t], RLP, fm[t], FM, up),
-                (3, (3, 0)[n], rlm[t], RLM, fp[t], FP, down),
+            for k, half, buf, base, dst, dbase, to in (
+                (1, 0, rlp[t], RLP, fm[t], FM, up),
+                (3, 2, rlm[t], RLM, fp[t], FP, down),
             ):
-                settle(buf.at[n], recv.at[t, base + n])
+                settle(buf.at[j], recv.at[t, base + j])
                 a1, a2 = rel(t, 0, k), rel(t, 1, j)
-                w[t][a1, a2] = w[t][a1, a2] + buf[n]
-                push(w[t].at[a1, a2], dst.at[j], send.at[t, 1], recv.at[t, dbase + j], to, core)
+                w[t][a1, a2, half : half + 2] = w[t][a1, a2, half : half + 2] + buf[j]
+                push(
+                    w[t].at[a1, a2, half : half + 2], dst.at[j, half : half + 2],
+                    send.at[t, 1], recv.at[t, dbase + j], to, core,
+                )
+    push(px, pxr, xs.at[0], xr.at[0], mate, core)
+    push(rx, rxr, xs.at[1], xr.at[1], mate, core)
 
     for j in (2, 3, 1, 0):
         for t in range(3):
             settle(fm[t].at[j], recv.at[t, FM + j])
             settle(fp[t].at[j], recv.at[t, FP + j])
             a1, a2 = rel(t, 0, 0), rel(t, 1, j)
-
-            def body(i, carry):
-                s1[t][j, i] = (w[t][a1, a2, i].astype(F32) + fm[t][j, i].astype(F32) + fp[t][j, i].astype(F32)).astype(BF16)
-                return carry
-
-            lax.fori_loop(0, 4, body, 0)
-            if j:
-                push(s1[t].at[j], r2[t].at[j - 1], send.at[t, 2], recv.at[t, SE + j - 1], moved(axes[t][1], j), core)
-
-    for t in range(3):
-        for j in range(3):
-            settle(r2[t].at[j], recv.at[t, SE + j])
-        for m in (2, 1, 3, 0):
+            for m in (2, 1, 3, 0):
+                a3 = rel(t, 2, m)
+                s1[t][j, a3] = (
+                    w[t][a1, a2, a3].astype(F32) + fm[t][j, a3].astype(F32) + fp[t][j, a3].astype(F32)
+                ).astype(BF16)
+                if j:
+                    push(
+                        s1[t].at[j, a3], r2[t].at[j - 1, a3],
+                        send.at[t, 2], recv.at[t, SE + 4 * (j - 1) + m], moved(axes[t][1], j), core,
+                    )
+
+    for m in (2, 1, 3, 0):
+        for t in range(3):
             a3 = rel(t, 2, m)
             total = s1[t][0, a3].astype(F32)
-            for j in range(3):
+            for j in (1, 2, 0):
+                settle(r2[t].at[j, a3], recv.at[t, SE + 4 * j + m])
                 total = total + r2[t][j, a3].astype(F32)
             if m:
                 s2[t][m - 1] = total.astype(BF16)
@@ -217,7 +222,7 @@
                 s3[t][...] = total
     for t in range(3):
         total = s3[t][...]
-        for m in range(3):
+        for m in (0, 2, 1):
             settle(r3[t].at[m], recv.at[t, TH + m])
             total = total + r3[t][m].astype(F32)
         s3[t][...] = total
@@ -227,61 +232,55 @@
     rq[...] = squares[0] + squares[1] + squares[2] + squares[3]
     push(rq, rqr, xs.at[2], xr.at[2], mate, core)
     sums = [jnp.sum(v, axis=0, keepdims=True) for v in squares]
-    eight = jnp.concatenate(sums + sums, axis=0)
-    row8 = lax.broadcasted_iota(jnp.int32, (8, 128), 0)
-    eight = jnp.where((row8 >= 4 * hi) & (row8 < 4 * hi + 4), eight, 0.0)
     mine = at["x"] * 2 + core
-    st1[mine, 0:8, :] = eight
-    st1[mine, 8:16, :] = rs[...]
-    n = 0
-    for k in range(4):
-        for flip in (0, 1):
-            if k or flip:
-                tc = core if not flip else 1 - core
-                push(st1.at[mine], st1.at[mine], t1s.at[0], t1r.at[n], moved("x", k), tc)
-                n += 1
-    n = 0
-    for k in range(4):
-        for flip in (0, 1):
-            if k or flip:
-                settle(st1.at[0], t1r.at[n])
-                n += 1
-    total = st1[0]
-    for i in range(1, 8):
-        total = total + st1[i]
-    for level, (axis, buf) in enumerate((("y", st2), ("z", st3))):
-        buf[at[axis]] = total
-        for k in (2, 1, 3):
-            push(buf.at[at[axis]], buf.at[at[axis]], t2s.at[level], t2r.at[level, k - 1], moved(axis, k), core)
-        for k in (1, 3, 2):
-            settle(buf.at[0], t2r.at[level, k - 1])
-        total = buf[0] + buf[1] + buf[2] + buf[3]
-
-    column_sums = total[0:8, :]
+    st1[mine] = jnp.concatenate(sums + [rs_row, jnp.zeros((3, 128), F32)], axis=0)
+    near_group = [(k, flip) for k in (2, 1, 3, 0) for flip in (1, 0) if k or flip]
+    for n, (k, flip) in enumerate(near_group):
+        push(st1.at[mine], st1.at[mine], t1s.at[0], t1r.at[n], moved("x", k), 1 - core if flip else core)
+
+    def added(buf, lo_slot, hi_slot):
+        terms = [buf[i] for i in range(lo_slot, hi_slot)]
+        while len(terms) > 1:
+            terms = [a + b for a, b in zip(terms[0::2], terms[1::2])]
+        return terms[0]
+
+    olds = []
+    for i in range(2):
+        settle((pxr, rxr)[i], xr.at[i])
+    for tile in range(4):
+        old = jnp.where(hi == 0, pf[:, tile * 128 : tile * 128 + 128], pf[:, 512 + tile * 128 : 640 + tile * 128])
+        olds.append(old + pxr[:, tile * 128 : tile * 128 + 128].astype(F32))
+    row_state = jnp.sum(rx[...] + rxr[...], axis=1, keepdims=True)
+
+    for n in range(7):
+        settle(st1.at[0], t1r.at[n])
+    slot = at["y"] * 4 + at["z"]
+    st2[slot] = added(st1, 0, 8)
+    far_group = [(i, j) for i in (2, 1, 3, 0) for j in (2, 1, 3, 0) if i or j]
+    for n, (i, j) in enumerate(far_group):
+        to = dict(moved("y", i), z=mod4(at["z"] + j))
+        push(st2.at[slot], st2.at[slot], t2s.at[0], t2r.at[n], to, core)
+    settle(rqr, xr.at[2])
+    row_square = jnp.sum(rq[...] + rqr[...], axis=1, keepdims=True)
+    for n in range(15):
+        settle(st2.at[0], t2r.at[n])
+    half0, half1 = added(st2, 0, 8), added(st2, 8, 16)
+
+    column_sums = jnp.concatenate([half0[0:4, :], half1[0:4, :]], axis=0)
     norm_square = jnp.sum(jnp.sum(column_sums, axis=0, keepdims=True), axis=1, keepdims=True)
-    rs_total = jnp.sum(total[8:9, :], axis=1, keepdims=True)
+    rs_total = jnp.sum(half0[4:5, :] + half1[4:5, :], axis=1, keepdims=True)
     factor = jnp.minimum(1.0, CLIP / jnp.sqrt(norm_square + 1e-06))
     square_factor = factor * factor
     column_next = BETA * cs[...] + (1.0 - BETA) * (square_factor * column_sums * (1.0 / D))
-    coln[...] = column_next
     row_average = (BETA / D) * rs_total + (1.0 - BETA) * (square_factor * norm_square * (1.0 / (D * KW)))
-
-    for i in range(3):
-        settle((pxr, rxr, rqr)[i], xr.at[i])
-    row_state = jnp.sum(rx[...] + rxr[...], axis=1, keepdims=True)
-    row_square = jnp.sum(rq[...] + rqr[...], axis=1, keepdims=True)
     row_next = BETA * row_state + (1.0 - BETA) * (square_factor * row_square * (1.0 / KW))
-    rown_line = jnp.sum(jnp.where(on_diag, jnp.broadcast_to(row_next, (56, 128)), 0.0), axis=0, keepdims=True)
-    rown[...] = rown_line[:, 0:28]
 
     mine_half = jnp.where(hi == 0, column_next[0:4, :], column_next[4:8, :])
     fresh = []
     for tile in range(4):
-        old = jnp.where(hi == 0, pf[:, tile * 128 : tile * 128 + 128], pf[:, 512 + tile * 128 : 640 + tile * 128])
-        old = old + pxr[:, tile * 128 : tile * 128 + 128].astype(F32)
         second = row_next * mine_half[tile : tile + 1, :] / row_average
         update = factor * tiles[tile] / jnp.sqrt(second)
-        fresh.append((old - STEP * update).astype(BF16))
+        fresh.append((olds[tile] - STEP * update).astype(BF16))
     for t in range(3):
         a1, a2, a3 = pos[t]
         own[t][a1, a2, a3, 0:56, :] = fresh[t]
@@ -292,37 +291,45 @@
         for k in (2, 1, 3):
             push(block, block, send.at[t, 4], recv.at[t, GT + k - 1], moved(axes[t][2], k), core)
 
-    def arrived(t, j):
-        sub = own[t].at[pos[t][0], rel(t, 1, j)]
-        push(sub, sub, send.at[t, 6], recv.at[t, GM + j], moved(axes[t][0], 1), core)
-        push(sub, sub, send.at[t, 6], recv.at[t, GP + j], moved(axes[t][0], 3), core)
-        push(sub, other[t].at[pos[t][0], rel(t, 1, j)], send.at[t, 7], recv.at[t, GC], at, 1 - core)
-
-    for t in range(3):
-        for k in (1, 3, 2):
-            settle(own[t].at[0, 0, 0], recv.at[t, GT + k - 1])
-        sub = own[t].at[pos[t][0], pos[t][1]]
-        for k in (2, 1, 3):
-            push(sub, sub, send.at[t, 5], recv.at[t, GS + k - 1], moved(axes[t][1], k), core)
-        arrived(t, 0)
+    def onward(t, block, j):
+        push(block, block, send.at[t, 6], recv.at[t, GM + j], moved(axes[t][0], 1), core)
+        push(block, block, send.at[t, 6], recv.at[t, GP + j], moved(axes[t][0], 3), core)
+
+    def across(t, a1, a2):
+        push(own[t].at[a1, a2], other[t].at[a1, a2], send.at[t, 7], recv.at[t, GC], at, 1 - core)
+
+    for m in (0, 1, 3, 2):
+        for t in range(3):
+            block = own[t].at[pos[t][0], pos[t][1], rel(t, 2, m)]
+            if m:
+                settle(block, recv.at[t, GT + (4 - m) - 1])
+            for k in (2, 1, 3):
+                push(block, block, send.at[t, 5], recv.at[t, GS + k - 1], moved(axes[t][1], k), core)
+            onward(t, block, 0)
+    for t in range(3):
+        across(t, pos[t][0], pos[t][1])
     for j in (1, 3, 2):
         for t in range(3):
-            settle(own[t].at[0, 0], recv.at[t, GS + (4 - j) - 1])
-            arrived(t, j)
+            sub = own[t].at[pos[t][0], rel(t, 1, j)]
+            settle(sub, recv.at[t, GS + (4 - j) - 1])
+            onward(t, sub, j)
+            across(t, pos[t][0], rel(t, 1, j))
 
     for j in (0, 1, 3, 2):
         for t in range(3):
-            for base, k, onward in ((GM, 3, 1), (GP, 1, 3)):
+            for base, k, shift in ((GM, 3, 1), (GP, 1, 3)):
                 sub = own[t].at[rel(t, 0, k), rel(t, 1, j)]
                 settle(sub, recv.at[t, base + j])
-                if (j in (0, 3)) == (onward == 1):
-                    push(sub, sub, send.at[t, 6], recv.at[t, GO + j], moved(axes[t][0], onward), core)
-                push(sub, other[t].at[rel(t, 0, k), rel(t, 1, j)], send.at[t, 7], recv.at[t, GC], at, 1 - core)
+                if (j in (0, 3)) == (shift == 1):
+                    push(sub, sub, send.at[t, 6], recv.at[t, GO + j], moved(axes[t][0], shift), core)
+                across(t, rel(t, 0, k), rel(t, 1, j))
+    coln[...] = column_next
+    rown_line = jnp.sum(jnp.where(on_diag, jnp.broadcast_to(row_next, (56, 128)), 0.0), axis=0, keepdims=True)
+    rown[...] = rown_line[:, 0:28]
     for j in (0, 1, 3, 2):
         for t in range(3):
-            sub = own[t].at[rel(t, 0, 2), rel(t, 1, j)]
-            settle(sub, recv.at[t, GO + j])
-            push(sub, other[t].at[rel(t, 0, 2), rel(t, 1, j)], send.at[t, 7], recv.at[t, GC], at, 1 - core)
+            settle(own[t].at[rel(t, 0, 2), rel(t, 1, j)], recv.at[t, GO + j])
+            across(t, rel(t, 0, 2), rel(t, 1, j))
 
     for h in (0, 1):
         here = dict(at, y=2 * h + lo)
@@ -345,8 +352,7 @@
     for i in range(3):
         settle((px, rx, rq)[i], xs.at[i])
     settle(st1.at[0:7], t1s.at[0])
-    for level, buf in enumerate((st2, st3)):
-        settle(buf.at[0:3], t2s.at[level])
+    settle(st2.at[0:15], t2s.at[0])
 
 
 def layout_kernel(*refs):
@@ -374,12 +380,15 @@
     vmem = pl.BlockSpec(memory_space=pltpu.VMEM)
     anywhere = pl.BlockSpec(memory_space=pl.ANY)
 
+    def hbm(v):
+        return pltpu.with_memory_space_constraint(v, pltpu.HBM)
+
     def local(grad_bucket, parameters, row_state, column_state):
         def three(*lead, dtype=BF16):
             return [pltpu.VMEM(lead + b, dtype) for b in block]
 
         scratch = (
-            three(4, 4, 4) + three(4, 4, 4) + three(2, 4) + three(2, 4) + three(4, 4) + three(4, 4) + three(4, 4)
+            three(4, 4, 4) + three(4, 4, 4) + three(4, 2) + three(4, 2) + three(4, 4) + three(4, 4) + three(4, 4)
             + three(3, 4) + three(3) + three(3) + three(dtype=F32)
             + [
                 pltpu.VMEM((28, KW), BF16), pltpu.VMEM((1, 28), F32), pltpu.VMEM((8, 128), F32), pltpu.VMEM((8, 128), F32),
@@ -387,11 +396,11 @@
                 pltpu.VMEM((56, 512), BF16), pltpu.VMEM((56, 512), BF16),
                 pltpu.VMEM((56, 128), F32), pltpu.VMEM((56, 128), F32),
                 pltpu.VMEM((56, 128), F32), pltpu.VMEM((56, 128), F32),
-                pltpu.VMEM((8, 16, 128), F32), pltpu.VMEM((4, 16, 128), F32), pltpu.VMEM((4, 16, 128), F32),
+                pltpu.VMEM((8, 8, 128), F32), pltpu.VMEM((16, 8, 128), F32),
                 pltpu.SemaphoreType.DMA((3, NRECV)), pltpu.SemaphoreType.DMA((3, NSEND)),
                 pltpu.SemaphoreType.DMA((3,)), pltpu.SemaphoreType.DMA((3,)),
                 pltpu.SemaphoreType.DMA((7,)), pltpu.SemaphoreType.DMA((1,)),
-                pltpu.SemaphoreType.DMA((2, 3)), pltpu.SemaphoreType.DMA((2,)),
+                pltpu.SemaphoreType.DMA((15,)), pltpu.SemaphoreType.DMA((1,)),
                 pltpu.SemaphoreType.DMA((3,)),
             ]
         )
@@ -412,9 +421,9 @@
             name="adafactor_step",
         )(
             grad_bucket.reshape(4, 2, 2, 4, 56, KW),
-            parameters.reshape(28, KW),
-            row_state,
-            column_state.reshape(8, 128),
+            hbm(parameters.reshape(28, KW)),
+            hbm(row_state),
+            hbm(column_state.reshape(8, 128)),
         )
         whole, newp, rown, coln = pl.pallas_call(
             layout_kernel,

time: 70.5 us -> 64.8 us (0.919)
  Pallas kernels: 67.4 us -> 64.1 us
  local copies, waits for them, and re-layouts: 2.17 us -> 0 us
    pallas_call x1, Pallas kernels: 64.5 us -> 61.1 us  [local(): pl.pallas_call(step_kernel, out_shape=part + part + small, in_specs=[pl.B...]
    unnamed x6 -> x0, local copies, waits for them, and re-layouts: 2.17 us -> none
where the time goes in v2:
time: 64.8 us; the launch traced here: 64.7 us
  Pallas kernels  64.1 us (99%)
    pallas_call x1, Pallas kernels, local(): pl.pallas_call(step_kernel, out_shape=part + part + small, in_specs=[pl.B...  61.1 us
    pallas_call x1, Pallas kernels, local(): pl.pallas_call(layout_kernel, out_shape=[jax.ShapeDtypeStruct((4, 2, 2, 4...  2.96 us

profile of v2, /device:TPU:1, one launch (start us, length us, event | category | flops | bytes accessed | tf_op | source)
XLA Modules:
  0.0 64.7 jit_solution(476003572158790403)
XLA Ops:
  0.6 61.1 %adafactor_step.1 = (bf16[4,4,4,80,128]{4,3,2,1,0:T(8,128)(2,1)S(1)}, bf16[4,4,4,72,128]{4,3,2,1,0:T(8,128)(2,1)S(1)}, bf16[4,4,4,72,128]{4,3,2,1,0:T(8,128)(2,1...) custom-call(bf16[4,2,2,4,56,1024]{5,4,3,2,1,0:T(8,128)(2,1)} %bitcas, ...), custom_call_target="tpu_custom_call" | custom-call | tf_op jit(solution)/shard_map/adafactor_step/pallas_call | solution.py:412
  61.8 3.0 %lay_out.1 = (bf16[4,2,2,4,56,1024]{5,4,3,2,1,0:T(8,128)(2,1)}, bf16[28,1024]{1,0:T(8,128)(2,1)}, f32[1,28]{1,0:T(1,128)}, f32[8,128]{1,0:T(8,128)}) custom-call(bf16[4,4,4,80,128]{4,3,2,1,0:T(8,128)(2,1)S(1)} %get-tuple-element.17.refs_0_, bf16[4,4,4,72,128]{4,3,2,1,0:T(8,128)(2,1)S(1)} %get-tuple-element.18.refs_1_, ...), custom_call_target="tpu_custom_call" | custom-call | tf_op jit(solution)/shard_map/lay_out/pallas_call | solution.py:428

commit v3 on v2

--- a/solution.py
+++ b/solution.py
@@ -20,9 +20,9 @@
 STRIP = ((0, 24), (24, 40), (40, 56))
 ROWS = tuple(56 + b - a for a, b in STRIP)
 LD, PR, RLP, RLM, FM, FP, SE, TH = 0, 4, 8, 12, 16, 20, 24, 36
-GT, GS, GM, GP, GO, GC = 39, 42, 45, 49, 53, 57
-NRECV = 58
-NSEND = 8
+GT, GS, GM, GP, GO, GC, PT, PS = 39, 42, 45, 49, 53, 57, 58, 61
+NRECV = 64
+NSEND = 10
 
 
 def mod4(v):
@@ -75,9 +75,9 @@
     newp, rown, coln = outs[6:9]
     it = iter(refs)
     take3 = lambda: [next(it) for _ in range(3)]
-    w, pr, rlp, rlm, fm, fp, s1, r2, s2, r3, s3 = (take3() for _ in range(11))
-    par, line, rs, cs, pf, px, pxr, rx, rxr, rq, rqr, st1, st2 = (next(it) for _ in range(13))
-    recv, send, xr, xs, t1r, t1s, t2r, t2s, near = (next(it) for _ in range(9))
+    w, pr, rlp, rlm, fm, fp, s1, r2, s2, r3, s3, sg, pg = (take3() for _ in range(13))
+    par, line, rs, cs, pf, px, pxr, st1, st2, rb, rn, rf, cf = (next(it) for _ in range(13))
+    recv, send, xr, xs, t1r, t1s, t2r, t2s, t3r, t3s, near = (next(it) for _ in range(11))
 
     at, lo, hi, core = where_am_i()
 
@@ -112,8 +112,9 @@
     for axis in "xyz":
         for k in (1, 3):
             pl.semaphore_signal(barrier, inc=1, device_id=device(moved(axis, k), core), device_id_type=MESH)
+    pl.semaphore_signal(barrier, inc=1, device_id=device(moved("y", 2), core), device_id_type=MESH)
     pl.semaphore_signal(barrier, inc=1, device_id=device(at, 1 - core), device_id_type=MESH)
-    pl.semaphore_wait(barrier, 7)
+    pl.semaphore_wait(barrier, 8)
 
     for k in (2, 1, 3, 0):
         for t in range(3):
@@ -141,9 +142,17 @@
     rs[...] = jnp.zeros_like(rs)
     rs[0:1, 0:28] = line[...]
     rs_row = rs[0:1, :]
-    rx[...] = jnp.where(on_diag & (lane_of < 28), jnp.broadcast_to(rs_row, (56, 128)), 0.0)
+    rs_column = jnp.sum(jnp.where(on_diag & (lane_of < 28), jnp.broadcast_to(rs_row, (56, 128)), 0.0), axis=1, keepdims=True)
+
+    def as_row(column):
+        return jnp.sum(jnp.where(row_of == lane_of, jnp.broadcast_to(column, (56, 128)), 0.0), axis=0, keepdims=True)
+
+    def as_column(row):
+        return jnp.sum(jnp.where(row_of == lane_of, jnp.broadcast_to(row, (56, 128)), 0.0), axis=1, keepdims=True)
+
+    rs_row = as_row(rs_column)
     px[...] = jnp.where(hi == 0, pf[:, 512:1024], pf[:, 0:512]).astype(BF16)
-    mate = moved("y", 2)
+    push(px, pxr, xs.at[0], xr.at[0], moved("y", 2), core)
 
     def add_chunk(t, a1):
         settle(w[t].at[a1], recv_k[0])
@@ -189,8 +198,6 @@
                     w[t].at[a1, a2, half : half + 2], dst.at[j, half : half + 2],
                     send.at[t, 1], recv.at[t, dbase + j], to, core,
                 )
-    push(px, pxr, xs.at[0], xr.at[0], mate, core)
-    push(rx, rxr, xs.at[1], xr.at[1], mate, core)
 
     for j in (2, 3, 1, 0):
         for t in range(3):
@@ -208,6 +215,29 @@
                         send.at[t, 2], recv.at[t, SE + 4 * (j - 1) + m], moved(axes[t][1], j), core,
                     )
 
+    settle(pxr, xr.at[0])
+    olds = []
+    for tile in range(4):
+        old = jnp.where(hi == 0, pf[:, tile * 128 : tile * 128 + 128], pf[:, 512 + tile * 128 : 640 + tile * 128])
+        olds.append((old + pxr[:, tile * 128 : tile * 128 + 128].astype(F32)).astype(BF16))
+
+    def spread(t, buf, ssem, base):
+        block = buf[t].at[pos[t][1], pos[t][2]]
+        for k in (2, 1, 3):
+            push(block, block, send.at[t, ssem], recv.at[t, base + k - 1], moved(axes[t][2], k), core)
+
+    def spread_on(t, buf, ssem, got, base):
+        for k in (1, 3, 2):
+            settle(buf[t].at[0, 0], recv.at[t, got + k - 1])
+        sub = buf[t].at[pos[t][1]]
+        for k in (2, 1, 3):
+            push(sub, sub, send.at[t, ssem], recv.at[t, base + k - 1], moved(axes[t][1], k), core)
+
+    for t in range(3):
+        pg[t][pos[t][1], pos[t][2], 0:56, :] = olds[t]
+        pg[t][pos[t][1], pos[t][2], 56 : ROWS[t], :] = olds[3][STRIP[t][0] : STRIP[t][1], :]
+        spread(t, pg, 8, PT)
+
     for m in (2, 1, 3, 0):
         for t in range(3):
             a3 = rel(t, 2, m)
@@ -221,22 +251,27 @@
             else:
                 s3[t][...] = total
     for t in range(3):
+        spread_on(t, pg, 9, PT, PS)
+    for t in range(3):
         total = s3[t][...]
         for m in (0, 2, 1):
             settle(r3[t].at[m], recv.at[t, TH + m])
             total = total + r3[t][m].astype(F32)
         s3[t][...] = total
+        sg[t][pos[t][1], pos[t][2]] = total.astype(BF16)
 
     tiles = [s3[t][0:56, :] for t in range(3)] + [jnp.concatenate([s3[t][56 : ROWS[t], :] for t in range(3)], axis=0)]
     squares = [v * v for v in tiles]
-    rq[...] = squares[0] + squares[1] + squares[2] + squares[3]
-    push(rq, rqr, xs.at[2], xr.at[2], mate, core)
+    row_squares = jnp.sum(squares[0] + squares[1] + squares[2] + squares[3], axis=1, keepdims=True)
     sums = [jnp.sum(v, axis=0, keepdims=True) for v in squares]
     mine = at["x"] * 2 + core
-    st1[mine] = jnp.concatenate(sums + [rs_row, jnp.zeros((3, 128), F32)], axis=0)
+    st1[mine] = jnp.concatenate(sums + [rs_row, as_row(row_squares), jnp.zeros((2, 128), F32)], axis=0)
     near_group = [(k, flip) for k in (2, 1, 3, 0) for flip in (1, 0) if k or flip]
     for n, (k, flip) in enumerate(near_group):
         push(st1.at[mine], st1.at[mine], t1s.at[0], t1r.at[n], moved("x", k), 1 - core if flip else core)
+
+    for t in range(3):
+        spread(t, sg, 4, GT)
 
     def added(buf, lo_slot, hi_slot):
         terms = [buf[i] for i in range(lo_slot, hi_slot)]
@@ -244,24 +279,18 @@
             terms = [a + b for a, b in zip(terms[0::2], terms[1::2])]
         return terms[0]
 
-    olds = []
-    for i in range(2):
-        settle((pxr, rxr)[i], xr.at[i])
-    for tile in range(4):
-        old = jnp.where(hi == 0, pf[:, tile * 128 : tile * 128 + 128], pf[:, 512 + tile * 128 : 640 + tile * 128])
-        olds.append(old + pxr[:, tile * 128 : tile * 128 + 128].astype(F32))
-    row_state = jnp.sum(rx[...] + rxr[...], axis=1, keepdims=True)
-
     for n in range(7):
         settle(st1.at[0], t1r.at[n])
     slot = at["y"] * 4 + at["z"]
     st2[slot] = added(st1, 0, 8)
+    rb[slot] = jnp.concatenate([st1[i, 5:6, :] for i in range(8)] + [st1[i, 4:5, :] for i in range(8)], axis=0)
     far_group = [(i, j) for i in (2, 1, 3, 0) for j in (2, 1, 3, 0) if i or j]
-    for n, (i, j) in enumerate(far_group):
-        to = dict(moved("y", i), z=mod4(at["z"] + j))
-        push(st2.at[slot], st2.at[slot], t2s.at[0], t2r.at[n], to, core)
-    settle(rqr, xr.at[2])
-    row_square = jnp.sum(rq[...] + rqr[...], axis=1, keepdims=True)
+    for buf, ssem, rsem in ((st2, t2s, t2r), (rb, t3s, t3r)):
+        for n, (i, j) in enumerate(far_group):
+            to = dict(moved("y", i), z=mod4(at["z"] + j))
+            push(buf.at[slot], buf.at[slot], ssem.at[0], rsem.at[n], to, core)
+    for t in range(3):
+        spread_on(t, sg, 5, GT, GS)
     for n in range(15):
         settle(st2.at[0], t2r.at[n])
     half0, half1 = added(st2, 0, 8), added(st2, 8, 16)
@@ -273,23 +302,31 @@
     square_factor = factor * factor
     column_next = BETA * cs[...] + (1.0 - BETA) * (square_factor * column_sums * (1.0 / D))
     row_average = (BETA / D) * rs_total + (1.0 - BETA) * (square_factor * norm_square * (1.0 / (D * KW)))
-    row_next = BETA * row_state + (1.0 - BETA) * (square_factor * row_square * (1.0 / KW))
-
-    mine_half = jnp.where(hi == 0, column_next[0:4, :], column_next[4:8, :])
-    fresh = []
-    for tile in range(4):
-        second = row_next * mine_half[tile : tile + 1, :] / row_average
-        update = factor * tiles[tile] / jnp.sqrt(second)
-        fresh.append((olds[tile] - STEP * update).astype(BF16))
-    for t in range(3):
-        a1, a2, a3 = pos[t]
-        own[t][a1, a2, a3, 0:56, :] = fresh[t]
-        own[t][a1, a2, a3, 56 : ROWS[t], :] = fresh[3][STRIP[t][0] : STRIP[t][1], :]
-
-    for t in range(3):
-        block = own[t].at[pos[t]]
-        for k in (2, 1, 3):
-            push(block, block, send.at[t, 4], recv.at[t, GT + k - 1], moved(axes[t][2], k), core)
+    cf[...] = STEP * factor * jnp.sqrt(row_average) / jnp.sqrt(column_next)
+    for n in range(15):
+        settle(rb.at[0], t3r.at[n])
+    for i in range(8):
+        both = rb[i] + rb[8 + i]
+        rn[i] = BETA * both[8:16, :] + (1.0 - BETA) * (square_factor * both[0:8, :] * (1.0 / KW))
+        rf[i] = 1.0 / jnp.sqrt(rn[i])
+
+    def update(t, j):
+        a2 = rel(t, 1, j)
+
+        def body(a3, carry):
+            here = {axes[t][0]: pos[t][0], axes[t][1]: a2, axes[t][2]: a3}
+            half = 4 * lax.div(here["y"], 2)
+            group = lax.rem(here["y"], 2) * 4 + here["z"]
+            scale = as_column(rf[group, pl.ds(here["x"] * 2 + core, 1), :])
+            new = sg[t][a2, a3].astype(F32)
+            old = pg[t][a2, a3].astype(F32)
+            own[t][pos[t][0], a2, a3, 0:56, :] = (old[0:56] - new[0:56] * (scale * cf[pl.ds(half + t, 1), :])).astype(BF16)
+            own[t][pos[t][0], a2, a3, 56 : ROWS[t], :] = (
+                old[56:] - new[56:] * (scale[STRIP[t][0] : STRIP[t][1]] * cf[pl.ds(half + 3, 1), :])
+            ).astype(BF16)
+            return carry
+
+        lax.fori_loop(0, 4, body, 0)
 
     def onward(t, block, j):
         push(block, block, send.at[t, 6], recv.at[t, GM + j], moved(axes[t][0], 1), core)
@@ -298,20 +335,13 @@
     def across(t, a1, a2):
         push(own[t].at[a1, a2], other[t].at[a1, a2], send.at[t, 7], recv.at[t, GC], at, 1 - core)
 
-    for m in (0, 1, 3, 2):
-        for t in range(3):
-            block = own[t].at[pos[t][0], pos[t][1], rel(t, 2, m)]
-            if m:
-                settle(block, recv.at[t, GT + (4 - m) - 1])
-            for k in (2, 1, 3):
-                push(block, block, send.at[t, 5], recv.at[t, GS + k - 1], moved(axes[t][1], k), core)
-            onward(t, block, 0)
-    for t in range(3):
-        across(t, pos[t][0], pos[t][1])
-    for j in (1, 3, 2):
-        for t in range(3):
+    for j in (0, 1, 3, 2):
+        for t in range(3):
+            if j:
+                settle(sg[t].at[0], recv.at[t, GS + (4 - j) - 1])
+                settle(pg[t].at[0], recv.at[t, PS + (4 - j) - 1])
+            update(t, j)
             sub = own[t].at[pos[t][0], rel(t, 1, j)]
-            settle(sub, recv.at[t, GS + (4 - j) - 1])
             onward(t, sub, j)
             across(t, pos[t][0], rel(t, 1, j))
 
@@ -324,8 +354,8 @@
                     push(sub, sub, send.at[t, 6], recv.at[t, GO + j], moved(axes[t][0], shift), core)
                 across(t, rel(t, 0, k), rel(t, 1, j))
     coln[...] = column_next
-    rown_line = jnp.sum(jnp.where(on_diag, jnp.broadcast_to(row_next, (56, 128)), 0.0), axis=0, keepdims=True)
-    rown[...] = rown_line[:, 0:28]
+    mine_row = rn[lo * 4 + at["z"], pl.ds(mine, 1), :]
+    rown[...] = jnp.where(hi == 0, mine_row[:, 0:28], mine_row[:, 28:56])
     for j in (0, 1, 3, 2):
         for t in range(3):
             settle(own[t].at[rel(t, 0, 2), rel(t, 1, j)], recv.at[t, GO + j])
@@ -348,11 +378,13 @@
         settle(w[t].at[0, 0:3], send.at[t, 5])
         settle(w[t].at[0:3], send.at[t, 6])
         settle(w[t], send.at[t, 7])
+        settle(w[t].at[0, 0, 0:3], send.at[t, 8])
+        settle(w[t].at[0, 0:3], send.at[t, 9])
         settle(other[t], recv.at[t, GC])
-    for i in range(3):
-        settle((px, rx, rq)[i], xs.at[i])
+    settle(px, xs.at[0])
     settle(st1.at[0:7], t1s.at[0])
     settle(st2.at[0:15], t2s.at[0])
+    settle(rb.at[0:15], t3s.at[0])
 
 
 def layout_kernel(*refs):
@@ -389,17 +421,17 @@
 
         scratch = (
             three(4, 4, 4) + three(4, 4, 4) + three(4, 2) + three(4, 2) + three(4, 4) + three(4, 4) + three(4, 4)
-            + three(3, 4) + three(3) + three(3) + three(dtype=F32)
+            + three(3, 4) + three(3) + three(3) + three(dtype=F32) + three(4, 4) + three(4, 4)
             + [
                 pltpu.VMEM((28, KW), BF16), pltpu.VMEM((1, 28), F32), pltpu.VMEM((8, 128), F32), pltpu.VMEM((8, 128), F32),
                 pltpu.VMEM((56, 1024), F32),
                 pltpu.VMEM((56, 512), BF16), pltpu.VMEM((56, 512), BF16),
-                pltpu.VMEM((56, 128), F32), pltpu.VMEM((56, 128), F32),
-                pltpu.VMEM((56, 128), F32), pltpu.VMEM((56, 128), F32),
-                pltpu.VMEM((8, 8, 128), F32), pltpu.VMEM((16, 8, 128), F32),
+                pltpu.VMEM((8, 8, 128), F32), pltpu.VMEM((16, 8, 128), F32), pltpu.VMEM((16, 16, 128), F32),
+                pltpu.VMEM((8, 8, 128), F32), pltpu.VMEM((8, 8, 128), F32), pltpu.VMEM((8, 128), F32),
                 pltpu.SemaphoreType.DMA((3, NRECV)), pltpu.SemaphoreType.DMA((3, NSEND)),
-                pltpu.SemaphoreType.DMA((3,)), pltpu.SemaphoreType.DMA((3,)),
+                pltpu.SemaphoreType.DMA((1,)), pltpu.SemaphoreType.DMA((1,)),
                 pltpu.SemaphoreType.DMA((7,)), pltpu.SemaphoreType.DMA((1,)),
+                pltpu.SemaphoreType.DMA((15,)), pltpu.SemaphoreType.DMA((1,)),
                 pltpu.SemaphoreType.DMA((15,)), pltpu.SemaphoreType.DMA((1,)),
                 pltpu.SemaphoreType.DMA((3,)),
             ]

time: 64.8 us -> 61.6 us (0.951)
  Pallas kernels: 64.1 us -> 60.8 us
    pallas_call x1, Pallas kernels: 61.1 us -> 57.9 us  [local(): pl.pallas_call(step_kernel, out_shape=part + part + small, in_specs=[pl.B...]
where the time goes in v3:
time: 61.6 us; the launch traced here: 61.5 us
  Pallas kernels  60.8 us (99%)
  between operations  0.64 us (1%)
    pallas_call x1, Pallas kernels, local(): pl.pallas_call(step_kernel, out_shape=part + part + small, in_specs=[pl.B...  57.9 us
    pallas_call x1, Pallas kernels, local(): pl.pallas_call(layout_kernel, out_shape=[jax.ShapeDtypeStruct((4, 2, 2, 4...  2.96 us

profile of v3, /device:TPU:1, one launch (start us, length us, event | category | flops | bytes accessed | tf_op | source)
XLA Modules:
  0.0 61.5 jit_solution(458865238079460620)
XLA Ops:
  0.6 57.9 %adafactor_step.1 = (bf16[4,4,4,80,128]{4,3,2,1,0:T(8,128)(2,1)S(1)}, bf16[4,4,4,72,128]{4,3,2,1,0:T(8,128)(2,1)S(1)}, bf16[4,4,4,72,128]{4,3,2,1,0:T(8,128)(2,1...) custom-call(bf16[4,2,2,4,56,1024]{5,4,3,2,1,0:T(8,128)(2,1)} %bitcas, ...), custom_call_target="tpu_custom_call" | custom-call | tf_op jit(solution)/shard_map/adafactor_step/pallas_call | solution.py:444
  58.5 3.0 %lay_out.1 = (bf16[4,2,2,4,56,1024]{5,4,3,2,1,0:T(8,128)(2,1)}, bf16[28,1024]{1,0:T(8,128)(2,1)}, f32[1,28]{1,0:T(1,128)}, f32[8,128]{1,0:T(8,128)}) custom-call(bf16[4,4,4,80,128]{4,3,2,1,0:T(8,128)(2,1)S(1)} %get-tuple-element.17.refs_0_, bf16[4,4,4,72,128]{4,3,2,1,0:T(8,128)(2,1)S(1)} %get-tuple-element.18.refs_1_, ...), custom_call_target="tpu_custom_call" | custom-call | tf_op jit(solution)/shard_map/lay_out/pallas_call | solution.py:460

commit v4 on v3

--- a/solution.py
+++ b/solution.py
@@ -103,10 +103,6 @@
     small = ((par_in, par), (rs_in, line), (cs_in, cs))
     for i, (src, dst) in enumerate(small):
         pltpu.make_async_copy(src, dst, near.at[i]).start()
-    for k in (2, 1, 3, 0):
-        for t in range(3):
-            for src, dst in copies(t, rel(t, 0, k), core, g, w[t]):
-                pltpu.make_async_copy(src, dst, recv.at[t, LD + k]).start()
 
     barrier = pltpu.get_barrier_semaphore()
     for axis in "xyz":
@@ -114,14 +110,22 @@
             pl.semaphore_signal(barrier, inc=1, device_id=device(moved(axis, k), core), device_id_type=MESH)
     pl.semaphore_signal(barrier, inc=1, device_id=device(moved("y", 2), core), device_id_type=MESH)
     pl.semaphore_signal(barrier, inc=1, device_id=device(at, 1 - core), device_id_type=MESH)
+    for k in (2,):
+        for t in range(3):
+            for src, dst in copies(t, rel(t, 0, k), core, g, w[t]):
+                pltpu.make_async_copy(src, dst, recv.at[t, LD + k]).start()
     pl.semaphore_wait(barrier, 8)
-
     for k in (2, 1, 3, 0):
         for t in range(3):
             for src, (_, dst) in zip(
                 [s for s, _ in copies(t, rel(t, 0, k), 1 - core, g, pr[t])], copies(t, rel(t, 0, k), core, g, pr[t])
             ):
                 push(src, dst, send.at[t, 0], recv.at[t, PR + k], at, 1 - core)
+    for k in (1, 3, 0):
+        for t in range(3):
+            for src, dst in copies(t, rel(t, 0, k), core, g, w[t]):
+                pltpu.make_async_copy(src, dst, recv.at[t, LD + k]).start()
+
 
     pf[...] = jnp.zeros_like(pf)
     for i, (src, dst) in enumerate(small):
@@ -150,7 +154,9 @@
     def as_column(row):
         return jnp.sum(jnp.where(row_of == lane_of, jnp.broadcast_to(row, (56, 128)), 0.0), axis=1, keepdims=True)
 
-    rs_row = as_row(rs_column)
+    rs_row = jnp.sum(
+        jnp.where(row_of == lane_of - 64, jnp.broadcast_to(rs_column, (56, 128)), 0.0), axis=0, keepdims=True
+    )
     px[...] = jnp.where(hi == 0, pf[:, 512:1024], pf[:, 0:512]).astype(BF16)
     push(px, pxr, xs.at[0], xr.at[0], moved("y", 2), core)
 
@@ -251,8 +257,6 @@
             else:
                 s3[t][...] = total
     for t in range(3):
-        spread_on(t, pg, 9, PT, PS)
-    for t in range(3):
         total = s3[t][...]
         for m in (0, 2, 1):
             settle(r3[t].at[m], recv.at[t, TH + m])
@@ -265,13 +269,15 @@
     row_squares = jnp.sum(squares[0] + squares[1] + squares[2] + squares[3], axis=1, keepdims=True)
     sums = [jnp.sum(v, axis=0, keepdims=True) for v in squares]
     mine = at["x"] * 2 + core
-    st1[mine] = jnp.concatenate(sums + [rs_row, as_row(row_squares), jnp.zeros((2, 128), F32)], axis=0)
+    st1[mine] = jnp.concatenate(sums + [rs_row, as_row(row_squares) + rs_row, jnp.zeros((2, 128), F32)], axis=0)
     near_group = [(k, flip) for k in (2, 1, 3, 0) for flip in (1, 0) if k or flip]
     for n, (k, flip) in enumerate(near_group):
         push(st1.at[mine], st1.at[mine], t1s.at[0], t1r.at[n], moved("x", k), 1 - core if flip else core)
 
     for t in range(3):
         spread(t, sg, 4, GT)
+    for t in range(3):
+        spread_on(t, pg, 9, PT, PS)
 
     def added(buf, lo_slot, hi_slot):
         terms = [buf[i] for i in range(lo_slot, hi_slot)]
@@ -283,7 +289,7 @@
         settle(st1.at[0], t1r.at[n])
     slot = at["y"] * 4 + at["z"]
     st2[slot] = added(st1, 0, 8)
-    rb[slot] = jnp.concatenate([st1[i, 5:6, :] for i in range(8)] + [st1[i, 4:5, :] for i in range(8)], axis=0)
+    rb[slot] = jnp.concatenate([st1[i, 5:6, :] for i in range(8)], axis=0)
     far_group = [(i, j) for i in (2, 1, 3, 0) for j in (2, 1, 3, 0) if i or j]
     for buf, ssem, rsem in ((st2, t2s, t2r), (rb, t3s, t3r)):
         for n, (i, j) in enumerate(far_group):
@@ -307,7 +313,7 @@
         settle(rb.at[0], t3r.at[n])
     for i in range(8):
         both = rb[i] + rb[8 + i]
-        rn[i] = BETA * both[8:16, :] + (1.0 - BETA) * (square_factor * both[0:8, :] * (1.0 / KW))
+        rn[i] = BETA * pltpu.roll(both, 64, 1) + (1.0 - BETA) * (square_factor * both * (1.0 / KW))
         rf[i] = 1.0 / jnp.sqrt(rn[i])
 
     def update(t, j):
@@ -426,7 +432,7 @@
                 pltpu.VMEM((28, KW), BF16), pltpu.VMEM((1, 28), F32), pltpu.VMEM((8, 128), F32), pltpu.VMEM((8, 128), F32),
                 pltpu.VMEM((56, 1024), F32),
                 pltpu.VMEM((56, 512), BF16), pltpu.VMEM((56, 512), BF16),
-                pltpu.VMEM((8, 8, 128), F32), pltpu.VMEM((16, 8, 128), F32), pltpu.VMEM((16, 16, 128), F32),
+                pltpu.VMEM((8, 8, 128), F32), pltpu.VMEM((16, 8, 128), F32), pltpu.VMEM((16, 8, 128), F32),
                 pltpu.VMEM((8, 8, 128), F32), pltpu.VMEM((8, 8, 128), F32), pltpu.VMEM((8, 128), F32),
                 pltpu.SemaphoreType.DMA((3, NRECV)), pltpu.SemaphoreType.DMA((3, NSEND)),
                 pltpu.SemaphoreType.DMA((1,)), pltpu.SemaphoreType.DMA((1,)),

time: 61.6 us -> 60.4 us (0.981)
  Pallas kernels: 60.8 us -> 59.6 us
    pallas_call x1, Pallas kernels: 57.9 us -> 56.7 us  [local(): pl.pallas_call(step_kernel, out_shape=part + part + small, in_specs=[pl.B...]
where the time goes in v4:
time: 60.4 us; the launch traced here: 60.3 us
  Pallas kernels  59.6 us (99%)
  between operations  0.64 us (1%)
    pallas_call x1, Pallas kernels, local(): pl.pallas_call(step_kernel, out_shape=part + part + small, in_specs=[pl.B...  56.7 us
    pallas_call x1, Pallas kernels, local(): pl.pallas_call(layout_kernel, out_shape=[jax.ShapeDtypeStruct((4, 2, 2, 4...  2.96 us

profile of v4, /device:TPU:1, one launch (start us, length us, event | category | flops | bytes accessed | tf_op | source)
XLA Modules:
  0.0 60.3 jit_solution(3980289883505942121)
XLA Ops:
  0.6 56.7 %adafactor_step.1 = (bf16[4,4,4,80,128]{4,3,2,1,0:T(8,128)(2,1)S(1)}, bf16[4,4,4,72,128]{4,3,2,1,0:T(8,128)(2,1)S(1)}, bf16[4,4,4,72,128]{4,3,2,1,0:T(8,128)(2,1...) custom-call(bf16[4,2,2,4,56,1024]{5,4,3,2,1,0:T(8,128)(2,1)} %bitcas, ...), custom_call_target="tpu_custom_call" | custom-call | tf_op jit(solution)/shard_map/adafactor_step/pallas_call | solution.py:450
  57.3 3.0 %lay_out.1 = (bf16[4,2,2,4,56,1024]{5,4,3,2,1,0:T(8,128)(2,1)}, bf16[28,1024]{1,0:T(8,128)(2,1)}, f32[1,28]{1,0:T(1,128)}, f32[8,128]{1,0:T(8,128)}) custom-call(bf16[4,4,4,80,128]{4,3,2,1,0:T(8,128)(2,1)S(1)} %get-tuple-element.17.refs_0_, bf16[4,4,4,72,128]{4,3,2,1,0:T(8,128)(2,1)S(1)} %get-tuple-element.18.refs_1_, ...), custom_call_target="tpu_custom_call" | custom-call | tf_op jit(solution)/shard_map/lay_out/pallas_call | solution.py:466

commit v5 on v4

--- a/solution.py
+++ b/solution.py
@@ -236,7 +236,7 @@
         for k in (1, 3, 2):
             settle(buf[t].at[0, 0], recv.at[t, got + k - 1])
         sub = buf[t].at[pos[t][1]]
-        for k in (2, 1, 3):
+        for k in (1, 3, 2):
             push(sub, sub, send.at[t, ssem], recv.at[t, base + k - 1], moved(axes[t][1], k), core)
 
     for t in range(3):
@@ -349,7 +349,8 @@
             update(t, j)
             sub = own[t].at[pos[t][0], rel(t, 1, j)]
             onward(t, sub, j)
-            across(t, pos[t][0], rel(t, 1, j))
+            if j == 2:
+                push(own[t].at[pos[t][0]], other[t].at[pos[t][0]], send.at[t, 7], recv.at[t, GC], at, 1 - core)
 
     for j in (0, 1, 3, 2):
         for t in range(3):

time: 60.4 us -> 60.2 us (level)
  no operation moved by 1% of the time
where the time goes in v5:
time: 60.2 us; the launch traced here: 60.1 us
  Pallas kernels  59.5 us (99%)
  between operations  0.64 us (1%)
    pallas_call x1, Pallas kernels, local(): pl.pallas_call(step_kernel, out_shape=part + part + small, in_specs=[pl.B...  56.5 us
    pallas_call x1, Pallas kernels, local(): pl.pallas_call(layout_kernel, out_shape=[jax.ShapeDtypeStruct((4, 2, 2, 4...  2.96 us

profile of v5, /device:TPU:1, one launch (start us, length us, event | category | flops | bytes accessed | tf_op | source)
XLA Modules:
  0.0 60.1 jit_solution(8007126669440753829)
XLA Ops:
  0.6 56.5 %adafactor_step.1 = (bf16[4,4,4,80,128]{4,3,2,1,0:T(8,128)(2,1)S(1)}, bf16[4,4,4,72,128]{4,3,2,1,0:T(8,128)(2,1)S(1)}, bf16[4,4,4,72,128]{4,3,2,1,0:T(8,128)(2,1...) custom-call(bf16[4,2,2,4,56,1024]{5,4,3,2,1,0:T(8,128)(2,1)} %bitcas, ...), custom_call_target="tpu_custom_call" | custom-call | tf_op jit(solution)/shard_map/adafactor_step/pallas_call | solution.py:451
  57.2 3.0 %lay_out.1 = (bf16[4,2,2,4,56,1024]{5,4,3,2,1,0:T(8,128)(2,1)}, bf16[28,1024]{1,0:T(8,128)(2,1)}, f32[1,28]{1,0:T(1,128)}, f32[8,128]{1,0:T(8,128)}) custom-call(bf16[4,4,4,80,128]{4,3,2,1,0:T(8,128)(2,1)S(1)} %get-tuple-element.17.refs_0_, bf16[4,4,4,72,128]{4,3,2,1,0:T(8,128)(2,1)S(1)} %get-tuple-element.18.refs_1_, ...), custom_call_target="tpu_custom_call" | custom-call | tf_op jit(solution)/shard_map/lay_out/pallas_call | solution.py:467
